TPU v7x, 128 devices: a whole 4x4x4 slice. The times are simulated.
128 devices in a mesh: gx: 32 (over x, y, core), gy: 4 (over z).
Axes of the slice: x: 4, y: 4, z: 4, core: 2. Of those that a mesh axis runs over, the one named last changes fastest.
Arguments:
- signals: float32 [64, 32, 16, 128], P('gx', 'gy'), may hold values from -6 to 6
- tiles: bfloat16 [64, 32, 4, 128, 128], P('gx', 'gy'), may hold values from 0 to 0.00390625
- tile_dir: int32 [64, 32, 4], P('gx', 'gy'), may hold values from 0 to 8
- tile_mask: int32 [64, 32, 4], P('gx', 'gy'), may hold values 0 or 1
- live_rows: int32 [64, 32], P('gx', 'gy'), may hold values from 32 to 128
- bound_rows: int32 [64, 32], P('gx', 'gy'), may hold values from 1 to 32, as said below
- scale_coeffs: float32 [6, 5], replicated, may hold values from -1 to 1
- spectral_bound: float32 [1], replicated, may hold values from 2.5 to 4
Outputs:
- coefficients: float32 [6, 64, 32, 16, 128], P(None, 'gx', 'gy')
- energy: float32 [6, 16], replicated
Inputs may be any that keep to these rules, and one draw needn't show every extreme that they name: `bound_rows`: in every draw, some blocks on every device have exactly 32 boundary rows.
All inputs are finite; a program needn't handle non-finite values. No bound on the sum of `tile_mask` on one device may be relied on, other than what follows from the above.
Results may differ from a plain program's by a relative error of at most 0.0003.
Values may be sent and summed in bfloat16 or wider, within the bound.
A program may use at most 64 MiB of HBM per device.

v0:
```python
import functools

import jax
import jax.numpy as jnp
from jax import lax
from jax.experimental import pallas as pl
from jax.experimental.pallas import tpu as pltpu
from jax.sharding import PartitionSpec as P

DEG = 4
VMEM_LIMIT = 67043328
EDGE = 32
MESH = pl.DeviceIdType.MESH
NT = (((1,), (1,)), ((), ()))


def kernel(
    nx, ny, sig_hbm, tiles_hbm, tdir_hbm, tmask_hbm, live_hbm, edge_hbm, coef_hbm, bound_hbm,
    totals_hbm, energy,
    totals, sig, tdir, tmask, live_rows, bound_rows, coef, bound, tiles, w_own, w_edge, own0, own, acc, cheb, slope, en_all, pads, x_out, x_in,
    tile_sem, send_sem, recv_sem, en_send, en_recv, in_sem, out_sem,
):
    ex, ey, chan, size = sig.shape
    slots = tiles.shape[2]
    scales = coef.shape[0]
    groups = size // EDGE
    n = nx * ny
    gx, gy = lax.axis_index("gx"), lax.axis_index("gy")
    me = gx * ny + gy
    blocks = [(i, j) for i in range(ex) for j in range(ey)]

    for r in range(DEG):
        pad = pads[r]
        for row in (0, ex + 1, ex + 2):
            pad[row] = jnp.zeros(pad.shape[1:], pad.dtype)
        for row in range(1, ex + 1):
            for col in (0, ey + 1):
                pad[row, col] = jnp.zeros(pad.shape[2:], pad.dtype)
        x_in[r][...] = jnp.zeros(x_in[r].shape, x_in[r].dtype)

    barrier = pltpu.get_barrier_semaphore()

    fetches = [
        pltpu.make_async_copy(src, dst, in_sem.at[k])
        for k, (src, dst) in enumerate(
            [
                (live_hbm, live_rows), (edge_hbm, bound_rows), (sig_hbm, sig), (tdir_hbm, tdir),
                (tmask_hbm, tmask), (coef_hbm, coef), (bound_hbm, bound),
            ]
        )
    ]
    for copy in fetches:
        copy.start()

    def others(act):
        def one(kx, px, ky):
            py = gy + ky
            act(kx * ny + ky, px, jnp.where(py >= ny, py - ny, py))

        for ky in range(1, ny):
            one(0, gx, ky)

        @pl.loop(1, nx)
        def _(kx):
            px = gx + kx
            px = jnp.where(px >= nx, px - nx, px)
            for ky in range(ny):
                one(kx, px, ky)

    def greet(k, px, py):
        pl.semaphore_signal(barrier, inc=1, device_id=(px, py), device_id_type=MESH)

    others(greet)

    def tile_copy(i, j):
        return pltpu.make_async_copy(
            tiles_hbm.at[i, j], tiles.at[i, j], tile_sem.at[i * ey + j]
        )

    for i, j in blocks:
        tile_copy(i, j).start()

    for copy in fetches:
        copy.wait()

    lane = lax.broadcasted_iota(jnp.int32, (1, size), 1)
    factor = 2.0 / jnp.full((1, size), bound[0, 0], jnp.float32)

    def live_of(i, j):
        return (lane < live_rows[i, j]).astype(jnp.float32)

    def edge_of(i, j):
        return (lane < bound_rows[i, j]).astype(jnp.float32)

    def spread(v, i, j):
        v = v * edge_of(i, j)
        step = EDGE
        while step < size:
            v = v + pltpu.roll(v, step, 1)
            step *= 2
        return v.astype(jnp.bfloat16)

    first_row = lax.broadcasted_iota(jnp.int32, (chan, size), 0) == 0
    for b, (i, j) in enumerate(blocks):
        live = live_of(i, j)
        v = sig[i, j] * live
        cheb[0, b] = v
        ind = jnp.where(first_row, jnp.broadcast_to(live, (chan, size)), 0.0)
        joined = jnp.concatenate([v, ind], axis=0)
        own0[b] = joined.astype(jnp.bfloat16)
        pads[0][i + 1, j + 1] = spread(joined, i, j)

    pl.semaphore_wait(barrier, n - 1)

    sides = []
    for dx in (-1, 0, 1):
        for dy in (-1, 0, 1):
            if dx or dy:
                sides.append((dx, dy))

    def cut(d, extent, far):
        if d == 0:
            return pl.ds(1, extent)
        if far:
            return pl.ds(extent + 1 if d < 0 else 0, 1)
        return pl.ds(1 if d < 0 else extent, 1)

    def inside(dx, dy):
        ok = None
        for d, g, m in ((dx, gx, nx), (dy, gy, ny)):
            if d:
                here = g > 0 if d < 0 else g < m - 1
                ok = here if ok is None else jnp.logical_and(ok, here)
        return ok

    def halo(r, k, dx, dy):
        pad = pads[r]
        if dy == 0:
            src = x_out[r].at[0 if dx < 0 else 1]
            dst = x_in[r].at[1 if dx < 0 else 0]
        else:
            src = pad.at[cut(dx, ex, False), cut(dy, ey, False)]
            dst = pad.at[cut(dx, ex, True), cut(dy, ey, True)]
        return pltpu.make_async_remote_copy(
            src_ref=src,
            dst_ref=dst,
            send_sem=send_sem.at[r, k],
            recv_sem=recv_sem.at[r, k],
            device_id=(gx + dx, gy + dy),
            device_id_type=MESH,
        )

    order = sorted(range(len(sides)), key=lambda k: -abs(sides[k][0]) - abs(sides[k][1]))
    corners = [(i, j) for i, j in blocks if i in (0, ex - 1) and j in (0, ey - 1)]
    inner = [(i, j) for i, j in blocks if (i, j) not in corners]

    def send(r, chosen):
        for k in order:
            dx, dy = sides[k]
            if not chosen(dx, dy):
                continue

            @pl.when(inside(dx, dy))
            def _():
                halo(r, k, dx, dy).start()

    def receive(r):
        for k in order:
            dx, dy = sides[k]

            @pl.when(inside(-dx, -dy))
            def _():
                halo(r, k, dx, dy).wait_recv()

    def group_of(s):
        return jnp.logical_and(lane >= s * EDGE, lane < (s + 1) * EDGE)

    def pack(r, side):
        row = 1 if side == 0 else ex
        for q in range(x_out[r].shape[1]):
            packed = None
            for t in range(min(groups, ey - q * groups)):
                term = pads[r][row, q * groups + t + 1] * group_of(t).astype(jnp.bfloat16)
                packed = term if packed is None else packed + term
            x_out[r][side, q] = packed

    def unpack(r):
        for side in (0, 1):
            for j in range(ey):
                v = x_in[r][side, j // groups].astype(jnp.float32)
                v = jnp.where(group_of(j % groups), v, 0.0)
                step = EDGE
                while step < size:
                    v = v + pltpu.roll(v, step, 1)
                    step *= 2
                pads[r][0 if side == 0 else ex + 1, j + 1] = v.astype(jnp.bfloat16)

    def add_totals(k):
        for s in range(scales):
            c = coef[s, k] * (0.5 if k == 0 else 1.0)
            for b, (i, j) in enumerate(blocks):
                term = c * cheb[k, b]
                totals[s, i, j] = term if k == 0 else totals[s, i, j] + term

    def weights(i, j):
        b = i * ey + j
        total = None
        packed = None
        for s in range(slots):
            tile = tiles[i, j, s].astype(jnp.float32)
            used = jnp.logical_and(tmask[i, s, j] == 1, tdir[i, s, j] == 4)
            term = tile * jnp.where(used, 1.0, 0.0)
            total = term if total is None else total + term
            rolled = pltpu.roll(tile, s * EDGE, 1) if s else tile
            packed = rolled if packed is None else jnp.where(lane >= s * EDGE, rolled, packed)
        high = total.astype(jnp.bfloat16)
        w_own[b, :, :size] = high
        w_own[b, :, size:] = (total - high.astype(jnp.float32)).astype(jnp.bfloat16)
        w_edge[b] = packed.astype(jnp.bfloat16)

    def gather(r, i, j):
        pad = pads[r]
        picked = None
        for s in range(slots):
            d = tdir[i, s, j]
            ok = jnp.logical_and(tmask[i, s, j] == 1, d != 4)
            row = (d * 11) >> 5
            col = d - 3 * row
            cell = pad[jnp.where(ok, row + i, ex + 2), jnp.where(ok, col + j, 0)]
            term = cell * group_of(s).astype(jnp.bfloat16)
            picked = term if picked is None else picked + term
        return picked

    send(0, lambda dx, dy: dy != 0)
    pack(0, 0)
    pack(0, 1)
    send(0, lambda dx, dy: dy == 0)
    for r in range(DEG):
        add_totals(r)
        for b, (i, j) in enumerate(blocks):
            if r == 0:
                tile_copy(i, j).wait()
                weights(i, j)
            mine = own0[b] if r == 0 else own[r - 1, b]
            acc[b, : mine.shape[0]] = lax.dot_general(
                jnp.concatenate([mine, mine], axis=1), w_own[b], NT,
                preferred_element_type=jnp.float32,
            )
        receive(r)
        unpack(r)
        for i, j in corners + inner:
            b = i * ey + j
            rows = 2 * chan if r == 0 else chan
            adj = acc[b, :rows] + lax.dot_general(
                gather(r, i, j), w_edge[b], NT, preferred_element_type=jnp.float32
            )
            scale = factor * live_of(i, j)
            v = cheb[r, b]
            if r == 0:
                slope[b] = scale * adj[chan : chan + 1] - 1.0
                following = slope[b] * v - scale * adj[:chan]
            else:
                following = 2.0 * (slope[b] * v - scale * adj) - cheb[r - 1, b]
            cheb[r + 1, b] = following
            if r < DEG - 1:
                own[r, b] = following.astype(jnp.bfloat16)
                pads[r + 1][i + 1, j + 1] = spread(following, i, j)
                if (i, j) == corners[-1]:
                    send(r + 1, lambda dx, dy: dy and (dx or ex <= 2))
                if (i, j) == inner[-1]:
                    pack(r + 1, 0)
                    pack(r + 1, 1)
                    send(r + 1, lambda dx, dy: not (dy and (dx or ex <= 2)))

    def out_copy(s):
        return pltpu.make_async_copy(totals.at[s], totals_hbm.at[s], out_sem.at[s])

    sums = []
    for s in range(scales):
        c = coef[s, DEG]
        part = jnp.zeros((chan, size), jnp.float32)
        for b, (i, j) in enumerate(blocks):
            t = totals[s, i, j] + c * cheb[DEG, b]
            totals[s, i, j] = t
            part = part + t * t
        sums.append(part)
        out_copy(s).start()

    width = en_all.shape[2]
    if width > scales * chan:
        sums.append(jnp.zeros((width - scales * chan, size), jnp.float32))
    local = lax.dot_general(
        jnp.ones((8, size), jnp.float32), jnp.concatenate(sums, axis=0), NT,
        precision=lax.Precision.HIGHEST, preferred_element_type=jnp.float32,
    )
    en_all[me] = local[:1]

    def share(k, slot, px, py):
        return pltpu.make_async_remote_copy(
            src_ref=en_all.at[slot],
            dst_ref=en_all.at[slot],
            send_sem=en_send.at[k],
            recv_sem=en_recv.at[slot],
            device_id=(px, py),
            device_id_type=MESH,
        )

    others(lambda k, px, py: share(k, me, px, py).start())
    others(lambda k, px, py: share(k, px * ny + py, px, py).wait_recv())

    total = jnp.sum(en_all[...], axis=0) * (1.0 / (ex * ey * size * n))
    for s in range(scales):
        energy[s : s + 1, :] = total[:, s * chan : (s + 1) * chan]

    others(lambda k, px, py: share(k, me, px, py).wait_send())

    for r in range(DEG):
        for k in order:
            dx, dy = sides[k]

            @pl.when(inside(dx, dy))
            def _():
                halo(r, k, dx, dy).wait_send()

    for s in range(scales):
        out_copy(s).wait()


def hand_out(made_hbm, energy_in, out_hbm, energy_out, held, held_energy, load_sem, store_sem):
    count = held.shape[0]
    loads = [
        pltpu.make_async_copy(made_hbm.at[s], held.at[s], load_sem.at[s]) for s in range(count)
    ] + [pltpu.make_async_copy(energy_in, held_energy, load_sem.at[count])]
    stores = [
        pltpu.make_async_copy(held.at[s], out_hbm.at[s], store_sem.at[s]) for s in range(count)
    ] + [pltpu.make_async_copy(held_energy, energy_out, store_sem.at[count])]
    for load in loads:
        load.start()
    for load, store in zip(loads, stores):
        load.wait()
        store.start()
    for store in stores:
        store.wait()


def solution(mesh):
    nx, ny = mesh.shape["gx"], mesh.shape["gy"]
    n = nx * ny

    def shards(
        signals, tiles, tile_dir, tile_mask, live_rows, bound_rows, scale_coeffs, spectral_bound
    ):
        ex, ey, chan, size = signals.shape
        slots = tiles.shape[2]
        scales = scale_coeffs.shape[0]
        nb = ex * ey
        width = -(-scales * chan // 128) * 128
        bf, f32 = jnp.bfloat16, jnp.float32
        vmem = pl.BlockSpec(memory_space=pltpu.VMEM)
        hbm = pl.BlockSpec(memory_space=pltpu.HBM)
        def packed():
            quads = -(-ey * EDGE // size)
            return [
                pltpu.VMEM((2, quads, chan * (2 if r == 0 else 1), size), bf) for r in range(DEG)
            ]

        made, energy = pl.pallas_call(
            functools.partial(kernel, nx, ny),
            out_shape=(
                jax.ShapeDtypeStruct((scales, ex, ey, chan, size), f32),
                jax.ShapeDtypeStruct((scales, chan), f32),
            ),
            in_specs=[hbm] * 8,
            out_specs=(hbm, vmem),
            scratch_shapes=[
                pltpu.VMEM((scales, ex, ey, chan, size), f32),
                pltpu.VMEM(signals.shape, f32),
                pltpu.SMEM((ex, slots, ey), jnp.int32),
                pltpu.SMEM((ex, slots, ey), jnp.int32),
                pltpu.SMEM((ex, ey), jnp.int32),
                pltpu.SMEM((ex, ey), jnp.int32),
                pltpu.SMEM(scale_coeffs.shape, f32),
                pltpu.SMEM((1, 1), f32),
                pltpu.VMEM((ex, ey, slots, size, size), bf),
                pltpu.VMEM((nb, size, 2 * size), bf),
                pltpu.VMEM((nb, size, size), bf),
                pltpu.VMEM((nb, 2 * chan, size), bf),
                pltpu.VMEM((DEG - 1, nb, chan, size), bf),
                pltpu.VMEM((nb, 2 * chan, size), f32),
                pltpu.VMEM((DEG + 1, nb, chan, size), f32),
                pltpu.VMEM((nb, 1, size), f32),
                pltpu.VMEM((n, 1, width), f32),
                [
                    pltpu.VMEM((ex + 3, ey + 2, chan * (2 if r == 0 else 1), size), bf)
                    for r in range(DEG)
                ],
                packed(),
                packed(),
                pltpu.SemaphoreType.DMA((nb,)),
                pltpu.SemaphoreType.DMA((DEG, 8)),
                pltpu.SemaphoreType.DMA((DEG, 8)),
                pltpu.SemaphoreType.DMA((n,)),
                pltpu.SemaphoreType.DMA((n,)),
                pltpu.SemaphoreType.DMA((8,)),
                pltpu.SemaphoreType.DMA((scales,)),
            ],
            compiler_params=pltpu.CompilerParams(
                collective_id=0, has_side_effects=True, vmem_limit_bytes=VMEM_LIMIT
            ),
        )(
            signals, tiles, jnp.swapaxes(tile_dir, 1, 2), jnp.swapaxes(tile_mask, 1, 2),
            live_rows, bound_rows, scale_coeffs, spectral_bound.reshape(1, 1),
        )
        return pl.pallas_call(
            hand_out,
            out_shape=(
                jax.ShapeDtypeStruct(made.shape, f32), jax.ShapeDtypeStruct(energy.shape, f32)
            ),
            in_specs=[hbm] * 2,
            out_specs=(hbm, hbm),
            scratch_shapes=[
                pltpu.VMEM(made.shape, f32),
                pltpu.VMEM(energy.shape, f32),
                pltpu.SemaphoreType.DMA((scales + 1,)),
                pltpu.SemaphoreType.DMA((scales + 1,)),
            ],
            compiler_params=pltpu.CompilerParams(vmem_limit_bytes=VMEM_LIMIT),
        )(made, energy)

    placed = (
        P("gx", "gy", None, None),
        P("gx", "gy", None, None, None),
        P("gx", "gy", None),
        P("gx", "gy", None),
        P("gx", "gy"),
        P("gx", "gy"),
        P(),
        P(),
    )
    return jax.shard_map(
        shards,
        mesh=mesh,
        in_specs=placed,
        out_specs=(P(None, "gx", "gy", None, None), P()),
        check_vma=False,
    )
```

profile of v0, /device:TPU:1, one launch (start us, length us, event | category | flops | bytes accessed | tf_op | source)
XLA Modules:
  0.0 41.0 jit_solution(3465112068861508622)
XLA Ops:
  1.3 37.7 %shard_map.95 = (f32[6,2,8,16,128]{4,3,2,1,0:T(8,128)}, f32[6,16]{1,0:T(8,128)}) custom-call(f32[2,8,16,128]{3,2,1,0:T(8,128)} %sig_hbm.1, bf16[2,8,4,128,128]{4,3,2,1,0:T(8,128)(2,1)} %tiles_hbm.1, s32[2,4,8]{2,1,0:T(4,128)} %bitcast.4, s32[2,4,8]{2,1,0:T(4,128)} %bitcast.5, s32[2,8]{1,0:T(2,128)} %live_hbm.1, s32[2,8]{1,0:T(2,128)} %edge_hbm.1, ...), custom_call_target="tpu_custom_call" | custom-call | tf_op jit(solution)/shard_map/pallas_call | solution.py:367
  39.0 2.0 %shard_map.96 = (f32[6,2,8,16,128]{4,3,2,1,0:T(8,128)}, f32[6,16]{1,0:T(8,128)}) custom-call(f32[6,2,8,16,128]{4,3,2,1,0:T(8,128)} %get-tuple-element.4.made_hbm, f32[6,16]{1,0:T(8,128)} %get-tuple-element.5.energy_in), custom_call_target="tpu_custom_call" | custom-call | tf_op jit(solution)/shard_map/pallas_call | solution.py:414
where the time goes:
time: 41.1 us; the launch traced here: 41 us
  Pallas kernels  39.7 us (97%)
  between operations  1.29 us (3%)
    pallas_call x1, Pallas kernels, shards(): pl.pallas_call(functools.partial(kernel, nx, ny), out_shape=(jax.ShapeDty...  37.7 us
    pallas_call x1, Pallas kernels, shards(): pl.pallas_call(hand_out, out_shape=(jax.ShapeDtypeStruct(made.shape, f32)...  1.99 us

commit v1 on v0

v1 whole, which is shorter than its diff:
```python
import functools

import jax
import jax.numpy as jnp
from jax import lax
from jax.experimental import pallas as pl
from jax.experimental.pallas import tpu as pltpu
from jax.sharding import PartitionSpec as P

DEG = 4
EDGE = 32
VMEM_LIMIT = 24 * 1024 * 1024
MESH = pl.DeviceIdType.MESH
NT = (((1,), (1,)), ((), ()))
SIDES = ((-1, 0), (1, 0), (0, -1), (0, 1), (-1, -1), (-1, 1), (1, -1), (1, 1))
X_BASE, Z_BASE, C_BASE, ZERO = 16, 32, 36, 40


def kernel(
    nx, ny, sig_hbm, tiles_hbm, tdir_hbm, tmask_hbm, live_hbm, edge_hbm, coef_hbm, bound,
    totals, en_in,
    sig, tdir, tmask, live_rows, bound_rows, coef, index, used, tiles, w_edge, own, acc,
    cheb, slope, scale, cells, x_out, x_in, z_in, c_in,
    in_sem, tile_sem, send_sem, recv_sem, en_sem,
):
    ex, ey, chan, size = sig.shape
    slots = tiles.shape[2]
    scales = coef.shape[0]
    groups = size // EDGE
    quads = ey // groups
    n = nx * ny
    bf, f32 = jnp.bfloat16, jnp.float32
    gx, gy = lax.axis_index("gx"), lax.axis_index("gy")
    me = gx * ny + gy
    corners = [(i, j) for j in (0, ey - 1) for i in range(ex)]
    inner = [(i, j) for j in range(1, ey - 1) for i in range(ex)]
    blocks = corners + inner

    fetches = [
        pltpu.make_async_copy(src, dst, in_sem.at[k])
        for k, (src, dst) in enumerate(
            [
                (sig_hbm, sig), (live_hbm, live_rows), (edge_hbm, bound_rows), (tdir_hbm, tdir),
                (tmask_hbm, tmask), (coef_hbm, coef),
            ]
        )
    ]
    for copy in fetches:
        copy.start()
    tile_groups = tile_sem.shape[0]
    span = ey // tile_groups

    def tile_copy(k):
        part = pl.ds(k * span, span)
        return pltpu.make_async_copy(tiles_hbm.at[:, part], tiles.at[:, part], tile_sem.at[k])

    for k in range(tile_groups):
        tile_copy(k).start()

    for r in range(DEG):
        for ref in (x_in[r], z_in[r], c_in[r]):
            ref[...] = jnp.zeros(ref.shape, ref.dtype)
    for k in range(len(cells)):
        cells[k][ZERO] = jnp.zeros(cells[k].shape[1:], bf)

    barrier = pltpu.get_barrier_semaphore()

    def others(act):
        def one(kx, px, ky):
            py = gy + ky
            act(kx * ny + ky, px, jnp.where(py >= ny, py - ny, py))

        for ky in range(1, ny):
            one(0, gx, ky)

        @pl.loop(1, nx)
        def _(kx):
            px = gx + kx
            px = jnp.where(px >= nx, px - nx, px)
            for ky in range(ny):
                one(kx, px, ky)

    def greet(k, px, py):
        pl.semaphore_signal(barrier, inc=1, device_id=(px, py), device_id_type=MESH)

    others(greet)

    def inside(dx, dy):
        ok = None
        for d, g, m in ((dx, gx, nx), (dy, gy, ny)):
            if d:
                here = g > 0 if d < 0 else g < m - 1
                ok = here if ok is None else jnp.logical_and(ok, here)
        return ok

    def flat(i, j):
        return j * ex + i

    for copy in fetches:
        copy.wait()

    lane = lax.broadcasted_iota(jnp.int32, (1, size), 1)
    factor = 2.0 / jnp.full((1, size), bound[0], f32)
    group = [
        jnp.logical_and(lane >= s * EDGE, lane < (s + 1) * EDGE).astype(bf) for s in range(groups)
    ]

    def live_of(i, j):
        return (lane < live_rows[i, j]).astype(f32)

    def spread(v, i, j):
        v = v * (lane < bound_rows[i, j]).astype(f32)
        step = EDGE
        while step < size:
            v = v + pltpu.roll(v, step, 1)
            step *= 2
        return v.astype(bf)

    first_row = lax.broadcasted_iota(jnp.int32, (chan, size), 0) == 0

    def prepare(i, j):
        b = flat(i, j)
        live = live_of(i, j)
        v = sig[i, j] * live
        cheb[0, b] = v
        ind = jnp.where(first_row, jnp.broadcast_to(live, (chan, size)), 0.0)
        joined = jnp.concatenate([v, ind], axis=0)
        own[0][b] = joined.astype(bf)
        cells[0][b] = spread(joined, i, j)

    def message(r, k):
        dx, dy = SIDES[k]
        now = cells[min(r, 1 + (r + 1) % 2)]
        x = 0 if dx < 0 else 1
        y = 0 if dy < 0 else 1
        if dy == 0:
            src, dst = x_out[r].at[x], x_in[r].at[1 - x]
        elif dx == 0:
            src, dst = now.at[pl.ds(flat(0, y * (ey - 1)), ex)], z_in[r].at[1 - y]
        else:
            src = now.at[flat(x * (ex - 1), y * (ey - 1))]
            dst = c_in[r].at[2 * (1 - x) + 1 - y]
        return pltpu.make_async_remote_copy(
            src_ref=src,
            dst_ref=dst,
            send_sem=send_sem.at[k],
            recv_sem=recv_sem.at[r % 2, k],
            device_id=(gx + dx, gy + dy),
            device_id_type=MESH,
        )

    def each(chosen, act, sign):
        for k in chosen:
            dx, dy = SIDES[k]

            @pl.when(inside(sign * dx, sign * dy))
            def _():
                act(k)

    x_sides, z_sides, c_sides = (0, 1), (2, 3), (4, 5, 6, 7)

    def send(r, chosen):
        each(chosen, lambda k: message(r, k).start(), 1)

    def sent(r):
        each(c_sides + z_sides + x_sides, lambda k: message(r, k).wait_send(), 1)

    def receive(r, chosen):
        each(chosen, lambda k: message(r, k).wait_recv(), -1)

    def cells_of(r):
        return cells[min(r, 1 + (r + 1) % 2)]

    def pack(r):
        for side in range(2):
            i = side * (ex - 1)
            for q in range(quads):
                packed = None
                for t in range(groups):
                    term = cells_of(r)[flat(i, q * groups + t)] * group[t]
                    packed = term if packed is None else packed + term
                x_out[r][side, q] = packed

    def unpack_x(r):
        for side in range(2):
            for q in range(quads):
                v = x_in[r][side, q]
                at = X_BASE + (side * quads + q) * groups
                cells_of(r)[at] = v
                v = v.astype(f32)
                for t in range(1, groups):
                    cells_of(r)[at + t] = pltpu.roll(v, t * EDGE, 1).astype(bf)

    def unpack_zc(r):
        for y in range(2):
            for i in range(ex):
                cells_of(r)[Z_BASE + y * ex + i] = z_in[r][y, i]
        for k in range(4):
            cells_of(r)[C_BASE + k] = c_in[r][k]

    def tables(i, j):
        b = flat(i, j)
        for s in range(slots):
            d = tdir[i, s, j]
            live = tmask[i, s, j] == 1
            row = (d * 11) >> 5
            ti = row + (i - 1)
            tj = d - 3 * row + (j - 1)
            at = tj * ex + ti
            up, down = ti < 0, ti > ex - 1
            at_x = X_BASE + (tj >> 2) * groups + ((s - tj) & 3)
            at = jnp.where(up, at_x, jnp.where(down, at_x + quads * groups, at))
            if j in (0, ey - 1):
                y = 0 if j == 0 else 1
                out = tj < 0 if j == 0 else tj > ey - 1
                at_z = Z_BASE + y * ex + ti
                at_z = jnp.where(up, C_BASE + y, jnp.where(down, C_BASE + 2 + y, at_z))
                at = jnp.where(out, at_z, at)
            mine = jnp.logical_and(live, d == 4)
            index[b * slots + s] = jnp.where(jnp.logical_and(live, d != 4), at, ZERO)
            used[b * slots + s] = jnp.where(mine, 1.0, 0.0)

    def weights(i, j):
        packed = None
        for s in range(slots):
            tile = tiles[i, j, s].astype(f32)
            rolled = pltpu.roll(tile, s * EDGE, 1) if s else tile
            packed = rolled if packed is None else jnp.where(lane >= s * EDGE, rolled, packed)
        w_edge[flat(i, j)] = packed.astype(bf)

    def own_product(r, i, j):
        b = flat(i, j)
        mine = own[min(r, 1)][b]
        total = None
        for s in range(0, slots, 2):
            pair = jnp.concatenate(
                [mine * used[b * slots + s + k].astype(bf) for k in range(2)], axis=1
            )
            tile = jnp.concatenate([tiles[i, j, s + k] for k in range(2)], axis=1)
            term = lax.dot_general(pair, tile, NT, preferred_element_type=f32)
            total = term if total is None else total + term
        if r == 0:
            acc[b] = total
        else:
            acc[b, :chan] = 2.0 * (slope[b] * cheb[r, b] - scale[b] * total) - cheb[r - 1, b]

    def edge_product(r, i, j):
        b = flat(i, j)
        picked = None
        for s in range(slots):
            term = cells_of(r)[index[b * slots + s]] * group[s]
            picked = term if picked is None else picked + term
        return lax.dot_general(picked, w_edge[b], NT, preferred_element_type=f32)

    def add_totals(k):
        for s in range(scales):
            c = coef[s, k] * (0.5 if k == 0 else 1.0)
            for i, j in blocks:
                term = c * cheb[k, flat(i, j)]
                totals[s, i, j] = term if k == 0 else totals[s, i, j] + term

    sums = [None] * scales

    def advance(r, i, j):
        b = flat(i, j)
        edge = edge_product(r, i, j)
        if r == 0:
            adj = acc[b] + edge
            s = factor * live_of(i, j)
            m = s * adj[chan : chan + 1] - 1.0
            scale[b] = s
            slope[b] = m
            following = m * cheb[0, b] - s * adj[:chan]
        else:
            following = acc[b, :chan] - (2.0 * scale[b]) * edge
        cheb[r + 1, b] = following
        if r < DEG - 1:
            own[1][b] = following.astype(bf)
            cells_of(r + 1)[b] = spread(following, i, j)
        else:
            for s in range(scales):
                t = totals[s, i, j] + coef[s, DEG] * following
                sums[s] = t * t if sums[s] is None else sums[s] + t * t

    for i, j in corners:
        prepare(i, j)
    for i, j in inner:
        prepare(i, j)
    pack(0)
    pl.semaphore_wait(barrier, n - 1)
    send(0, c_sides)
    send(0, z_sides)
    send(0, x_sides)
    for i, j in blocks:
        tables(i, j)
    for r in range(DEG):
        if r == 0:
            for k in range(tile_groups):
                tile_copy(k).wait()
            for i, j in blocks:
                weights(i, j)
        for i, j in blocks:
            own_product(r, i, j)
        add_totals(r)
        sent(r)
        receive(r, x_sides)
        unpack_x(r)
        for i, j in inner:
            advance(r, i, j)
        receive(r, z_sides + c_sides)
        unpack_zc(r)
        for i, j in corners:
            advance(r, i, j)
        if r < DEG - 1:
            send(r + 1, c_sides)
            send(r + 1, z_sides)
            pack(r + 1)
            send(r + 1, x_sides)

    width = en_in.shape[2]
    if width > scales * chan:
        sums.append(jnp.zeros((width - scales * chan, size), f32))
    stacked = jnp.concatenate(sums, axis=0)
    high = stacked.astype(bf)
    low = (stacked - high.astype(f32)).astype(bf)
    local = lax.dot_general(
        jnp.ones((chan, 2 * size), bf), jnp.concatenate([high, low], axis=1), NT,
        preferred_element_type=f32,
    )
    en_in[me] = local[:1]

    def share(k, px, py):
        return pltpu.make_async_remote_copy(
            src_ref=en_in.at[me],
            dst_ref=en_in.at[me],
            send_sem=en_sem.at[0],
            recv_sem=en_sem.at[1],
            device_id=(px, py),
            device_id_type=MESH,
        )

    others(lambda k, px, py: share(k, px, py).start())

    for s in range(scales):
        c = coef[s, DEG]
        for i, j in blocks:
            totals[s, i, j] = totals[s, i, j] + c * cheb[DEG, flat(i, j)]

    rest = en_in.at[pl.ds(0, n - 1)]
    pltpu.make_async_copy(rest, rest, en_sem.at[1]).wait()
    pltpu.make_async_copy(rest, rest, en_sem.at[0]).wait()


def hand_out(count, made, shared, out_hbm, energy_out, energy, sem):
    scales, ex, ey, chan, size = made.shape
    stores = [
        pltpu.make_async_copy(made.at[s], out_hbm.at[s], sem.at[s]) for s in range(scales)
    ]
    for store in stores:
        store.start()
    total = jnp.sum(shared[...], axis=0) * (1.0 / count)
    for s in range(scales):
        energy[s : s + 1, :] = total[:, s * chan : (s + 1) * chan]
    stores.append(pltpu.make_async_copy(energy, energy_out, sem.at[scales]))
    stores[-1].start()
    for store in stores:
        store.wait()


def solution(mesh):
    nx, ny = mesh.shape["gx"], mesh.shape["gy"]
    n = nx * ny

    def shards(
        signals, tiles, tile_dir, tile_mask, live_rows, bound_rows, scale_coeffs, spectral_bound
    ):
        ex, ey, chan, size = signals.shape
        slots = tiles.shape[2]
        scales = scale_coeffs.shape[0]
        nb = ex * ey
        width = -(-scales * chan // 128) * 128
        quads = ey * EDGE // size
        bf, f32 = jnp.bfloat16, jnp.float32
        vmem = pl.BlockSpec(memory_space=pltpu.VMEM)
        hbm = pl.BlockSpec(memory_space=pltpu.HBM)
        rows = [chan * (2 if r == 0 else 1) for r in range(DEG)]
        made, shared = pl.pallas_call(
            functools.partial(kernel, nx, ny),
            out_shape=(
                jax.ShapeDtypeStruct((scales, ex, ey, chan, size), f32),
                jax.ShapeDtypeStruct((n, 1, width), f32),
            ),
            in_specs=[hbm] * 7 + [pl.BlockSpec(memory_space=pltpu.SMEM)],
            out_specs=(vmem, vmem),
            scratch_shapes=[
                pltpu.VMEM(signals.shape, f32),
                pltpu.SMEM((ex, slots, ey), jnp.int32),
                pltpu.SMEM((ex, slots, ey), jnp.int32),
                pltpu.SMEM((ex, ey), jnp.int32),
                pltpu.SMEM((ex, ey), jnp.int32),
                pltpu.SMEM(scale_coeffs.shape, f32),
                pltpu.SMEM((nb * slots,), jnp.int32),
                pltpu.SMEM((nb * slots,), f32),
                pltpu.VMEM((ex, ey, slots, size, size), bf),
                pltpu.VMEM((nb, size, size), bf),
                [pltpu.VMEM((nb, 2 * chan, size), bf), pltpu.VMEM((nb, chan, size), bf)],
                pltpu.VMEM((nb, 2 * chan, size), f32),
                pltpu.VMEM((DEG + 1, nb, chan, size), f32),
                pltpu.VMEM((nb, 1, size), f32),
                pltpu.VMEM((nb, 1, size), f32),
                [pltpu.VMEM((ZERO + 1, rows[min(k, 1)], size), bf) for k in range(3)],
                [pltpu.VMEM((2, quads, rows[r], size), bf) for r in range(DEG)],
                [pltpu.VMEM((2, quads, rows[r], size), bf) for r in range(DEG)],
                [pltpu.VMEM((2, ex, rows[r], size), bf) for r in range(DEG)],
                [pltpu.VMEM((4, rows[r], size), bf) for r in range(DEG)],
                pltpu.SemaphoreType.DMA((6,)),
                pltpu.SemaphoreType.DMA((4,)),
                pltpu.SemaphoreType.DMA((8,)),
                pltpu.SemaphoreType.DMA((2, 8)),
                pltpu.SemaphoreType.DMA((2,)),
            ],
            compiler_params=pltpu.CompilerParams(
                collective_id=0, has_side_effects=True, vmem_limit_bytes=VMEM_LIMIT
            ),
        )(
            *[
                pltpu.with_memory_space_constraint(a, pltpu.HBM)
                for a in (
                    signals, tiles, jnp.swapaxes(tile_dir, 1, 2), jnp.swapaxes(tile_mask, 1, 2),
                    live_rows, bound_rows, scale_coeffs,
                )
            ], spectral_bound
        )
        return pl.pallas_call(
            functools.partial(hand_out, n * nb * size),
            out_shape=(
                jax.ShapeDtypeStruct(made.shape, f32),
                jax.ShapeDtypeStruct((scales, chan), f32),
            ),
            in_specs=[vmem] * 2,
            out_specs=(hbm, hbm),
            scratch_shapes=[
                pltpu.VMEM((scales, chan), f32),
                pltpu.SemaphoreType.DMA((scales + 1,)),
            ],
            compiler_params=pltpu.CompilerParams(vmem_limit_bytes=VMEM_LIMIT),
        )(made, shared)

    placed = (
        P("gx", "gy", None, None),
        P("gx", "gy", None, None, None),
        P("gx", "gy", None),
        P("gx", "gy", None),
        P("gx", "gy"),
        P("gx", "gy"),
        P(),
        P(),
    )
    return jax.shard_map(
        shards,
        mesh=mesh,
        in_specs=placed,
        out_specs=(P(None, "gx", "gy", None, None), P()),
        check_vma=False,
    )
```

time: 41.1 us -> 35.2 us (0.86)
  Pallas kernels: 39.7 us -> 33.8 us
    pallas_call x1, Pallas kernels: 37.7 us -> 32.7 us  [shards(): pl.pallas_call(functools.partial(kernel, nx, ny), out_shape=(jax.ShapeDty...]
    pallas_call x1, Pallas kernels: 1.99 us -> 1.04 us  [shards(): pl.pallas_call(functools.partial(hand_out, n * nb * size), out_shape=(jax...]
where the time goes in v1:
time: 35.2 us; the launch traced here: 35.1 us
  Pallas kernels  33.8 us (96%)
  between operations  1.29 us (4%)
    pallas_call x1, Pallas kernels, shards(): pl.pallas_call(functools.partial(kernel, nx, ny), out_shape=(jax.ShapeDty...  32.7 us
    pallas_call x1, Pallas kernels, shards(): pl.pallas_call(functools.partial(hand_out, n * nb * size), out_shape=(jax...  1.04 us

profile of v1, /device:TPU:1, one launch (start us, length us, event | category | flops | bytes accessed | tf_op | source)
XLA Modules:
  0.0 35.1 jit_solution(1090054285069598566)
XLA Ops:
  1.3 32.7 %shard_map.95 = (f32[6,2,8,16,128]{4,3,2,1,0:T(8,128)S(1)}, f32[128,1,128]{2,1,0:T(1,128)S(1)}) custom-call(f32[2,8,16,128]{3,2,1,0:T(8,128)} %sig_hbm.1, bf16[2,8,4,128,128]{4,3,2,1,0:T(8,128)(2,1)} %tiles_hbm.1, s32[2,4,8]{2,1,0:T(4,128)} %bitcast.2, s32[2,4,8]{2,1,0:T(4,128)} %bitcast.3, s32[2,8]{1,0:T(2,128)} %live_hbm.1, s32[2,8]{1,0:T(2,128)} %edge_hbm.1, ...), custom_call_target="tpu_custom_call" | custom-call | tf_op jit(solution)/shard_map/pallas_call | solution.py:387
  34.0 1.0 %shard_map.96 = (f32[6,2,8,16,128]{4,3,2,1,0:T(8,128)}, f32[6,16]{1,0:T(8,128)}) custom-call(f32[6,2,8,16,128]{4,3,2,1,0:T(8,128)S(1)} %get-tuple-element.4.made, f32[128,1,128]{2,1,0:T(1,128)S(1)} %get-tuple-element.5.shared), custom_call_target="tpu_custom_call" | custom-call | tf_op jit(solution)/shard_map/pallas_call | solution.py:434

commit v2 on v1

--- a/solution.py
+++ b/solution.py
@@ -13,6 +13,8 @@
 MESH = pl.DeviceIdType.MESH
 NT = (((1,), (1,)), ((), ()))
 SIDES = ((-1, 0), (1, 0), (0, -1), (0, 1), (-1, -1), (-1, 1), (1, -1), (1, 1))
+FAR = 4
+JUMPS = ((-4, 4), (-8, 8), (16,))
 X_BASE, Z_BASE, C_BASE, ZERO = 16, 32, 36, 40
 
 
@@ -20,8 +22,8 @@
     nx, ny, sig_hbm, tiles_hbm, tdir_hbm, tmask_hbm, live_hbm, edge_hbm, coef_hbm, bound,
     totals, en_in,
     sig, tdir, tmask, live_rows, bound_rows, coef, index, used, tiles, w_edge, own, acc,
-    cheb, slope, scale, cells, x_out, x_in, z_in, c_in,
-    in_sem, tile_sem, send_sem, recv_sem, en_sem,
+    copies, cheb, slope, scale, cells, x_out, x_in, z_in, c_in,
+    in_sem, tile_sem, send_sem, recv_sem, en_sem, know_sem,
 ):
     ex, ey, chan, size = sig.shape
     slots = tiles.shape[2]
@@ -65,25 +67,14 @@
 
     barrier = pltpu.get_barrier_semaphore()
 
-    def others(act):
-        def one(kx, px, ky):
-            py = gy + ky
-            act(kx * ny + ky, px, jnp.where(py >= ny, py - ny, py))
-
-        for ky in range(1, ny):
-            one(0, gx, ky)
-
-        @pl.loop(1, nx)
-        def _(kx):
-            px = gx + kx
-            px = jnp.where(px >= nx, px - nx, px)
-            for ky in range(ny):
-                one(kx, px, ky)
-
-    def greet(k, px, py):
-        pl.semaphore_signal(barrier, inc=1, device_id=(px, py), device_id_type=MESH)
-
-    others(greet)
+    def around(dx, dy):
+        px, py = gx + dx, gy + dy
+        px = jnp.where(px >= nx, px - nx, jnp.where(px < 0, px + nx, px)) if dx else px
+        py = jnp.where(py >= ny, py - ny, py) if dy else py
+        return px, py
+
+    def signal(semaphore, device):
+        pl.semaphore_signal(semaphore, inc=1, device_id=device, device_id_type=MESH)
 
     def inside(dx, dy):
         ok = None
@@ -96,25 +87,47 @@
     def flat(i, j):
         return j * ex + i
 
-    for copy in fetches:
+    for dx in (-1, 1):
+        for dy in (-1, 0, 1):
+
+            @pl.when(inside(dx, dy))
+            def _():
+                signal(barrier, (gx + dx, gy + dy))
+
+    for dy in range(1, ny):
+        signal(barrier, around(0, dy))
+    for dx in (-FAR, FAR):
+        signal(barrier, around(dx, 0))
+
+    def near(g, m):
+        return (g > 0).astype(jnp.int32) + (g < m - 1).astype(jnp.int32)
+
+    greeted = near(gx, nx) * (1 + near(gy, ny)) + (ny - 1) + 2
+
+    fetches[0].wait()
+    for copy in fetches[1:3]:
         copy.wait()
 
     lane = lax.broadcasted_iota(jnp.int32, (1, size), 1)
-    factor = 2.0 / jnp.full((1, size), bound[0], f32)
     group = [
         jnp.logical_and(lane >= s * EDGE, lane < (s + 1) * EDGE).astype(bf) for s in range(groups)
     ]
 
+    def repeats_of(i, j):
+        return ((lane & (EDGE - 1)) < bound_rows[i, j]).astype(f32)
+
     def live_of(i, j):
         return (lane < live_rows[i, j]).astype(f32)
 
-    def spread(v, i, j):
-        v = v * (lane < bound_rows[i, j]).astype(f32)
+    def repeat(v):
         step = EDGE
         while step < size:
             v = v + pltpu.roll(v, step, 1)
             step *= 2
-        return v.astype(bf)
+        return v
+
+    def edge_of(i, j):
+        return (lane < bound_rows[i, j]).astype(f32)
 
     first_row = lax.broadcasted_iota(jnp.int32, (chan, size), 0) == 0
 
@@ -123,10 +136,10 @@
         live = live_of(i, j)
         v = sig[i, j] * live
         cheb[0, b] = v
-        ind = jnp.where(first_row, jnp.broadcast_to(live, (chan, size)), 0.0)
-        joined = jnp.concatenate([v, ind], axis=0)
-        own[0][b] = joined.astype(bf)
-        cells[0][b] = spread(joined, i, j)
+        own[0][b, :chan] = v.astype(bf)
+        own[0][b, chan:] = jnp.where(first_row, live, 0.0).astype(bf)
+        cells[0][b, :chan] = repeat((v * edge_of(i, j)).astype(bf))
+        cells[0][b, chan:] = jnp.where(first_row, repeats_of(i, j), 0.0).astype(bf)
 
     def message(r, k):
         dx, dy = SIDES[k]
@@ -187,9 +200,8 @@
                 v = x_in[r][side, q]
                 at = X_BASE + (side * quads + q) * groups
                 cells_of(r)[at] = v
-                v = v.astype(f32)
                 for t in range(1, groups):
-                    cells_of(r)[at + t] = pltpu.roll(v, t * EDGE, 1).astype(bf)
+                    cells_of(r)[at + t] = pltpu.roll(v, t * EDGE, 1)
 
     def unpack_zc(r):
         for y in range(2):
@@ -223,10 +235,12 @@
     def weights(i, j):
         packed = None
         for s in range(slots):
-            tile = tiles[i, j, s].astype(f32)
-            rolled = pltpu.roll(tile, s * EDGE, 1) if s else tile
-            packed = rolled if packed is None else jnp.where(lane >= s * EDGE, rolled, packed)
-        w_edge[flat(i, j)] = packed.astype(bf)
+            tile = tiles[i, j, s]
+            term = (pltpu.roll(tile, s * EDGE, 1) if s else tile) * group[s]
+            packed = term if packed is None else packed + term
+        w_edge[flat(i, j), :size] = packed
+        for t in range(groups):
+            w_edge[flat(i, j), pl.ds(size + t * EDGE, EDGE)] = packed[:EDGE]
 
     def own_product(r, i, j):
         b = flat(i, j)
@@ -240,9 +254,14 @@
             term = lax.dot_general(pair, tile, NT, preferred_element_type=f32)
             total = term if total is None else total + term
         if r == 0:
-            acc[b] = total
+            acc[b, : 2 * chan] = total
+            acc[b, 2 * chan :] = repeat(total * edge_of(i, j))
+            copies[b] = repeat(cheb[0, b] * edge_of(i, j))
         else:
-            acc[b, :chan] = 2.0 * (slope[b] * cheb[r, b] - scale[b] * total) - cheb[r - 1, b]
+            base = 2.0 * (slope[b] * cheb[r, b] - scale[b] * total) - cheb[r - 1, b]
+            acc[b, :chan] = base
+            if r < DEG - 1:
+                acc[b, 2 * chan : 3 * chan] = repeat(base * edge_of(i, j))
 
     def edge_product(r, i, j):
         b = flat(i, j)
@@ -250,7 +269,8 @@
         for s in range(slots):
             term = cells_of(r)[index[b * slots + s]] * group[s]
             picked = term if picked is None else picked + term
-        return lax.dot_general(picked, w_edge[b], NT, preferred_element_type=f32)
+        weight = w_edge[b] if r < DEG - 1 else w_edge[b, :size]
+        return lax.dot_general(picked, weight, NT, preferred_element_type=f32)
 
     def add_totals(k):
         for s in range(scales):
@@ -265,18 +285,24 @@
         b = flat(i, j)
         edge = edge_product(r, i, j)
         if r == 0:
-            adj = acc[b] + edge
+            adj = acc[b, : 2 * chan] + edge[:, :size]
             s = factor * live_of(i, j)
             m = s * adj[chan : chan + 1] - 1.0
             scale[b] = s
             slope[b] = m
             following = m * cheb[0, b] - s * adj[:chan]
+            adj = acc[b, 2 * chan :] + edge[:, size:]
+            s = factor * repeats_of(i, j)
+            m = s * adj[chan : chan + 1] - 1.0
+            cells_of(r + 1)[b] = (m * copies[b] - s * adj[:chan]).astype(bf)
         else:
-            following = acc[b, :chan] - (2.0 * scale[b]) * edge
+            following = acc[b, :chan] - (2.0 * scale[b]) * edge[:, :size]
+            if r < DEG - 1:
+                far = acc[b, 2 * chan : 3 * chan] - (2.0 * factor * repeats_of(i, j)) * edge[:, size:]
+                cells_of(r + 1)[b] = far.astype(bf)
         cheb[r + 1, b] = following
         if r < DEG - 1:
             own[1][b] = following.astype(bf)
-            cells_of(r + 1)[b] = spread(following, i, j)
         else:
             for s in range(scales):
                 t = totals[s, i, j] + coef[s, DEG] * following
@@ -287,10 +313,13 @@
     for i, j in inner:
         prepare(i, j)
     pack(0)
-    pl.semaphore_wait(barrier, n - 1)
+    pl.semaphore_wait(barrier, greeted)
     send(0, c_sides)
     send(0, z_sides)
     send(0, x_sides)
+    for copy in fetches[3:]:
+        copy.wait()
+    factor = 2.0 / jnp.full((1, size), bound[0], f32)
     for i, j in blocks:
         tables(i, j)
     for r in range(DEG):
@@ -302,12 +331,17 @@
         for i, j in blocks:
             own_product(r, i, j)
         add_totals(r)
+        receive(r, x_sides)
         sent(r)
-        receive(r, x_sides)
         unpack_x(r)
         for i, j in inner:
             advance(r, i, j)
         receive(r, z_sides + c_sides)
+        if r > 0:
+            pl.semaphore_wait(know_sem.at[r - 1], len(JUMPS[r - 1]))
+        if r < len(JUMPS):
+            for dx in JUMPS[r]:
+                signal(know_sem.at[r], around(dx, 0))
         unpack_zc(r)
         for i, j in corners:
             advance(r, i, j)
@@ -329,7 +363,7 @@
     )
     en_in[me] = local[:1]
 
-    def share(k, px, py):
+    def share(px, py):
         return pltpu.make_async_remote_copy(
             src_ref=en_in.at[me],
             dst_ref=en_in.at[me],
@@ -339,7 +373,16 @@
             device_id_type=MESH,
         )
 
-    others(lambda k, px, py: share(k, px, py).start())
+    for py in range(ny):
+
+        @pl.when(gy != py)
+        def _():
+            share(gx, py).start()
+
+        @pl.loop(1, nx, unroll=True)
+        def _(kx):
+            px = gx + kx
+            share(jnp.where(px >= nx, px - nx, px), py).start()
 
     for s in range(scales):
         c = coef[s, DEG]
@@ -352,16 +395,13 @@
 
 
 def hand_out(count, made, shared, out_hbm, energy_out, energy, sem):
-    scales, ex, ey, chan, size = made.shape
-    stores = [
-        pltpu.make_async_copy(made.at[s], out_hbm.at[s], sem.at[s]) for s in range(scales)
-    ]
-    for store in stores:
-        store.start()
+    scales, chan = energy.shape
+    stores = [pltpu.make_async_copy(made, out_hbm, sem.at[0])]
+    stores[0].start()
     total = jnp.sum(shared[...], axis=0) * (1.0 / count)
     for s in range(scales):
         energy[s : s + 1, :] = total[:, s * chan : (s + 1) * chan]
-    stores.append(pltpu.make_async_copy(energy, energy_out, sem.at[scales]))
+    stores.append(pltpu.make_async_copy(energy, energy_out, sem.at[1]))
     stores[-1].start()
     for store in stores:
         store.wait()
@@ -402,9 +442,10 @@
                 pltpu.SMEM((nb * slots,), jnp.int32),
                 pltpu.SMEM((nb * slots,), f32),
                 pltpu.VMEM((ex, ey, slots, size, size), bf),
-                pltpu.VMEM((nb, size, size), bf),
+                pltpu.VMEM((nb, 2 * size, size), bf),
                 [pltpu.VMEM((nb, 2 * chan, size), bf), pltpu.VMEM((nb, chan, size), bf)],
-                pltpu.VMEM((nb, 2 * chan, size), f32),
+                pltpu.VMEM((nb, 4 * chan, size), f32),
+                pltpu.VMEM((nb, chan, size), f32),
                 pltpu.VMEM((DEG + 1, nb, chan, size), f32),
                 pltpu.VMEM((nb, 1, size), f32),
                 pltpu.VMEM((nb, 1, size), f32),
@@ -418,6 +459,7 @@
                 pltpu.SemaphoreType.DMA((8,)),
                 pltpu.SemaphoreType.DMA((2, 8)),
                 pltpu.SemaphoreType.DMA((2,)),
+                pltpu.SemaphoreType.REGULAR((len(JUMPS),)),
             ],
             compiler_params=pltpu.CompilerParams(
                 collective_id=0, has_side_effects=True, vmem_limit_bytes=VMEM_LIMIT
@@ -441,7 +483,7 @@
             out_specs=(hbm, hbm),
             scratch_shapes=[
                 pltpu.VMEM((scales, chan), f32),
-                pltpu.SemaphoreType.DMA((scales + 1,)),
+                pltpu.SemaphoreType.DMA((2,)),
             ],
             compiler_params=pltpu.CompilerParams(vmem_limit_bytes=VMEM_LIMIT),
         )(made, shared)

time: 35.2 us -> 32 us (0.909)
  Pallas kernels: 33.8 us -> 30.6 us
    pallas_call x1, Pallas kernels: 32.7 us -> 29.7 us  [shards(): pl.pallas_call(functools.partial(kernel, nx, ny), out_shape=(jax.ShapeDty...]
where the time goes in v2:
time: 32 us; the launch traced here: 31.9 us
  Pallas kernels  30.6 us (96%)
  between operations  1.29 us (4%)
    pallas_call x1, Pallas kernels, shards(): pl.pallas_call(functools.partial(kernel, nx, ny), out_shape=(jax.ShapeDty...  29.7 us
    pallas_call x1, Pallas kernels, shards(): pl.pallas_call(functools.partial(hand_out, n * nb * size), out_shape=(jax...  0.91 us

profile of v2, /device:TPU:1, one launch (start us, length us, event | category | flops | bytes accessed | tf_op | source)
XLA Modules:
  0.0 31.9 jit_solution(7547625956961979131)
XLA Ops:
  1.3 29.7 %shard_map.95 = (f32[6,2,8,16,128]{4,3,2,1,0:T(8,128)S(1)}, f32[128,1,128]{2,1,0:T(1,128)S(1)}) custom-call(f32[2,8,16,128]{3,2,1,0:T(8,128)} %sig_hbm.1, bf16[2,8,4,128,128]{4,3,2,1,0:T(8,128)(2,1)} %tiles_hbm.1, s32[2,4,8]{2,1,0:T(4,128)} %bitcast.2, s32[2,4,8]{2,1,0:T(4,128)} %bitcast.3, s32[2,8]{1,0:T(2,128)} %live_hbm.1, s32[2,8]{1,0:T(2,128)} %edge_hbm.1, ...), custom_call_target="tpu_custom_call" | custom-call | tf_op jit(solution)/shard_map/pallas_call | solution.py:427
  30.9 0.9 %shard_map.96 = (f32[6,2,8,16,128]{4,3,2,1,0:T(8,128)}, f32[6,16]{1,0:T(8,128)}) custom-call(f32[6,2,8,16,128]{4,3,2,1,0:T(8,128)S(1)} %get-tuple-element.4.made, f32[128,1,128]{2,1,0:T(1,128)S(1)} %get-tuple-element.5.shared), custom_call_target="tpu_custom_call" | custom-call | tf_op jit(solution)/shard_map/pallas_call | solution.py:476

commit v3 on v2

--- a/solution.py
+++ b/solution.py
@@ -13,8 +13,8 @@
 MESH = pl.DeviceIdType.MESH
 NT = (((1,), (1,)), ((), ()))
 SIDES = ((-1, 0), (1, 0), (0, -1), (0, 1), (-1, -1), (-1, 1), (1, -1), (1, 1))
-FAR = 4
-JUMPS = ((-4, 4), (-8, 8), (16,))
+STEPS = (2, 4, 8, 16)
+GROUPS = 2
 X_BASE, Z_BASE, C_BASE, ZERO = 16, 32, 36, 40
 
 
@@ -22,13 +22,14 @@
     nx, ny, sig_hbm, tiles_hbm, tdir_hbm, tmask_hbm, live_hbm, edge_hbm, coef_hbm, bound,
     totals, en_in,
     sig, tdir, tmask, live_rows, bound_rows, coef, index, used, tiles, w_edge, own, acc,
-    copies, cheb, slope, scale, cells, x_out, x_in, z_in, c_in,
-    in_sem, tile_sem, send_sem, recv_sem, en_sem, know_sem,
+    copies, cheb, slope, scale, cells, x_out, x_in, zc_in,
+    in_sem, send_sem, recv_sem, en_sem, know_sem,
 ):
     ex, ey, chan, size = sig.shape
     slots = tiles.shape[2]
     scales = coef.shape[0]
     groups = size // EDGE
+    wide = own[0].shape[1]
     quads = ey // groups
     n = nx * ny
     bf, f32 = jnp.bfloat16, jnp.float32
@@ -38,43 +39,15 @@
     inner = [(i, j) for j in range(1, ey - 1) for i in range(ex)]
     blocks = corners + inner
 
-    fetches = [
-        pltpu.make_async_copy(src, dst, in_sem.at[k])
-        for k, (src, dst) in enumerate(
-            [
-                (sig_hbm, sig), (live_hbm, live_rows), (edge_hbm, bound_rows), (tdir_hbm, tdir),
-                (tmask_hbm, tmask), (coef_hbm, coef),
-            ]
-        )
-    ]
-    for copy in fetches:
-        copy.start()
-    tile_groups = tile_sem.shape[0]
-    span = ey // tile_groups
-
-    def tile_copy(k):
-        part = pl.ds(k * span, span)
-        return pltpu.make_async_copy(tiles_hbm.at[:, part], tiles.at[:, part], tile_sem.at[k])
-
-    for k in range(tile_groups):
-        tile_copy(k).start()
-
-    for r in range(DEG):
-        for ref in (x_in[r], z_in[r], c_in[r]):
-            ref[...] = jnp.zeros(ref.shape, ref.dtype)
-    for k in range(len(cells)):
-        cells[k][ZERO] = jnp.zeros(cells[k].shape[1:], bf)
-
-    barrier = pltpu.get_barrier_semaphore()
-
-    def around(dx, dy):
-        px, py = gx + dx, gy + dy
-        px = jnp.where(px >= nx, px - nx, jnp.where(px < 0, px + nx, px)) if dx else px
-        py = jnp.where(py >= ny, py - ny, py) if dy else py
-        return px, py
-
-    def signal(semaphore, device):
-        pl.semaphore_signal(semaphore, inc=1, device_id=device, device_id_type=MESH)
+    def landing(r, k):
+        dx, dy = SIDES[k]
+        x = 0 if dx < 0 else 1
+        y = 0 if dy < 0 else 1
+        if dy == 0:
+            return x_in[r].at[x]
+        if dx == 0:
+            return zc_in[r].at[pl.ds(y * ex, ex)]
+        return zc_in[r].at[pl.ds(2 * ex + 2 * x + y, 1)]
 
     def inside(dx, dy):
         ok = None
@@ -84,28 +57,62 @@
                 ok = here if ok is None else jnp.logical_and(ok, here)
         return ok
 
+    def signal(semaphore, device):
+        pl.semaphore_signal(semaphore, inc=1, device_id=device, device_id_type=MESH)
+
     def flat(i, j):
         return j * ex + i
 
-    for dx in (-1, 1):
-        for dy in (-1, 0, 1):
-
-            @pl.when(inside(dx, dy))
+    fetches = [
+        pltpu.make_async_copy(src, dst, in_sem.at[k])
+        for src, dst, k in (
+            (sig_hbm, sig, 0), (live_hbm, live_rows, 1), (edge_hbm, bound_rows, 1),
+            (tdir_hbm, tdir, 2), (tmask_hbm, tmask, 2), (coef_hbm, coef, 2),
+        )
+    ]
+    span = ey // GROUPS
+    for k in range(GROUPS):
+        part = pl.ds(k * span, span)
+        fetches.append(
+            pltpu.make_async_copy(tiles_hbm.at[:, part], tiles.at[:, part], in_sem.at[3 + k])
+        )
+    def near(g, m, step=1):
+        return (g >= step).astype(jnp.int32) + (g < m - step).astype(jnp.int32)
+
+    def tell(k):
+        for dx in (-STEPS[k], STEPS[k]):
+
+            @pl.when(gx >= -dx if dx < 0 else gx < nx - dx)
             def _():
-                signal(barrier, (gx + dx, gy + dy))
-
-    for dy in range(1, ny):
-        signal(barrier, around(0, dy))
-    for dx in (-FAR, FAR):
-        signal(barrier, around(dx, 0))
-
-    def near(g, m):
-        return (g > 0).astype(jnp.int32) + (g < m - 1).astype(jnp.int32)
-
-    greeted = near(gx, nx) * (1 + near(gy, ny)) + (ny - 1) + 2
-
-    fetches[0].wait()
-    for copy in fetches[1:3]:
+                signal(know_sem.at[k], (gx + dx, gy))
+
+    def hear(k):
+        pl.semaphore_wait(know_sem.at[k], near(gx, nx, STEPS[k]))
+
+    greeted = (1 + near(gx, nx)) * (1 + near(gy, ny)) - 1
+    for copy in fetches[:3]:
+        copy.start()
+    barrier = pltpu.get_barrier_semaphore()
+    for dx, dy in SIDES:
+
+        @pl.when(inside(dx, dy))
+        def _():
+            signal(barrier, (gx + dx, gy + dy))
+
+    for copy in fetches[3:]:
+        copy.start()
+    for k, (dx, dy) in enumerate(SIDES):
+
+        @pl.when(jnp.logical_not(inside(dx, dy)))
+        def _():
+            for r in range(DEG):
+                part = landing(r, k)
+                part[...] = jnp.zeros(part.shape, bf)
+
+    for k in range(len(cells)):
+        cells[k][ZERO] = jnp.zeros(cells[k].shape[1:], bf)
+
+    for copy in fetches[:3]:
         copy.wait()
 
     lane = lax.broadcasted_iota(jnp.int32, (1, size), 1)
@@ -129,7 +136,7 @@
     def edge_of(i, j):
         return (lane < bound_rows[i, j]).astype(f32)
 
-    first_row = lax.broadcasted_iota(jnp.int32, (chan, size), 0) == 0
+    first_row = lax.broadcasted_iota(jnp.int32, (wide - chan, size), 0) == 0
 
     def prepare(i, j):
         b = flat(i, j)
@@ -143,43 +150,61 @@
 
     def message(r, k):
         dx, dy = SIDES[k]
-        now = cells[min(r, 1 + (r + 1) % 2)]
         x = 0 if dx < 0 else 1
         y = 0 if dy < 0 else 1
         if dy == 0:
-            src, dst = x_out[r].at[x], x_in[r].at[1 - x]
+            src = x_out[r].at[x]
         elif dx == 0:
-            src, dst = now.at[pl.ds(flat(0, y * (ey - 1)), ex)], z_in[r].at[1 - y]
+            src = cells_of(r).at[pl.ds(flat(0, y * (ey - 1)), ex)]
         else:
-            src = now.at[flat(x * (ex - 1), y * (ey - 1))]
-            dst = c_in[r].at[2 * (1 - x) + 1 - y]
+            src = cells_of(r).at[pl.ds(flat(x * (ex - 1), y * (ey - 1)), 1)]
         return pltpu.make_async_remote_copy(
             src_ref=src,
-            dst_ref=dst,
-            send_sem=send_sem.at[k],
-            recv_sem=recv_sem.at[r % 2, k],
+            dst_ref=landing(r, SIDES.index((-dx, -dy))),
+            send_sem=send_sem.at[0],
+            recv_sem=recv_sem.at[r % 2, 0 if dy == 0 else 1],
             device_id=(gx + dx, gy + dy),
             device_id_type=MESH,
         )
 
-    def each(chosen, act, sign):
+    x_sides, z_sides, c_sides = (0, 1), (2, 3), (4, 5, 6, 7)
+
+    def send(r, chosen):
         for k in chosen:
-            dx, dy = SIDES[k]
-
-            @pl.when(inside(sign * dx, sign * dy))
+
+            @pl.when(inside(*SIDES[k]))
             def _():
-                act(k)
-
-    x_sides, z_sides, c_sides = (0, 1), (2, 3), (4, 5, 6, 7)
-
-    def send(r, chosen):
-        each(chosen, lambda k: message(r, k).start(), 1)
+                message(r, k).start()
+
+    x_both = jnp.logical_and(gx > 0, gx < nx - 1)
+    y_both = jnp.logical_and(gy > 0, gy < ny - 1)
+
+    def await_parts(ref, sem, counts):
+        for xb in (True, False):
+            for yb in (True, False):
+                x_is = x_both if xb else jnp.logical_not(x_both)
+                y_is = y_both if yb else jnp.logical_not(y_both)
+                part = ref.at[pl.ds(0, counts(1 + xb, 1 + yb))]
+
+                @pl.when(jnp.logical_and(x_is, y_is))
+                def _():
+                    pltpu.make_async_copy(part, part, sem).wait()
 
     def sent(r):
-        each(c_sides + z_sides + x_sides, lambda k: message(r, k).wait_send(), 1)
-
-    def receive(r, chosen):
-        each(chosen, lambda k: message(r, k).wait_recv(), -1)
+        await_parts(
+            cells_of(r), send_sem.at[0], lambda xs, ys: quads * xs + ex * ys + xs * ys
+        )
+
+    def receive_x(r):
+        for xb in (True, False):
+            part = x_in[r].at[pl.ds(0, 1 + xb)]
+
+            @pl.when(x_both if xb else jnp.logical_not(x_both))
+            def _():
+                pltpu.make_async_copy(part, part, recv_sem.at[r % 2, 0]).wait()
+
+    def receive_zc(r):
+        await_parts(zc_in[r], recv_sem.at[r % 2, 1], lambda xs, ys: ex * ys + xs * ys)
 
     def cells_of(r):
         return cells[min(r, 1 + (r + 1) % 2)]
@@ -204,11 +229,7 @@
                     cells_of(r)[at + t] = pltpu.roll(v, t * EDGE, 1)
 
     def unpack_zc(r):
-        for y in range(2):
-            for i in range(ex):
-                cells_of(r)[Z_BASE + y * ex + i] = z_in[r][y, i]
-        for k in range(4):
-            cells_of(r)[C_BASE + k] = c_in[r][k]
+        cells_of(r)[pl.ds(Z_BASE, 2 * ex + 4)] = zc_in[r][...]
 
     def tables(i, j):
         b = flat(i, j)
@@ -254,14 +275,14 @@
             term = lax.dot_general(pair, tile, NT, preferred_element_type=f32)
             total = term if total is None else total + term
         if r == 0:
-            acc[b, : 2 * chan] = total
-            acc[b, 2 * chan :] = repeat(total * edge_of(i, j))
+            acc[b, :wide] = total
+            acc[b, wide:] = repeat(total * edge_of(i, j))
             copies[b] = repeat(cheb[0, b] * edge_of(i, j))
         else:
             base = 2.0 * (slope[b] * cheb[r, b] - scale[b] * total) - cheb[r - 1, b]
             acc[b, :chan] = base
             if r < DEG - 1:
-                acc[b, 2 * chan : 3 * chan] = repeat(base * edge_of(i, j))
+                acc[b, wide : wide + chan] = repeat(base * edge_of(i, j))
 
     def edge_product(r, i, j):
         b = flat(i, j)
@@ -285,20 +306,20 @@
         b = flat(i, j)
         edge = edge_product(r, i, j)
         if r == 0:
-            adj = acc[b, : 2 * chan] + edge[:, :size]
+            adj = acc[b, :wide] + edge[:, :size]
             s = factor * live_of(i, j)
             m = s * adj[chan : chan + 1] - 1.0
             scale[b] = s
             slope[b] = m
             following = m * cheb[0, b] - s * adj[:chan]
-            adj = acc[b, 2 * chan :] + edge[:, size:]
+            adj = acc[b, wide:] + edge[:, size:]
             s = factor * repeats_of(i, j)
             m = s * adj[chan : chan + 1] - 1.0
             cells_of(r + 1)[b] = (m * copies[b] - s * adj[:chan]).astype(bf)
         else:
             following = acc[b, :chan] - (2.0 * scale[b]) * edge[:, :size]
             if r < DEG - 1:
-                far = acc[b, 2 * chan : 3 * chan] - (2.0 * factor * repeats_of(i, j)) * edge[:, size:]
+                far = acc[b, wide : wide + chan] - (2.0 * factor * repeats_of(i, j)) * edge[:, size:]
                 cells_of(r + 1)[b] = far.astype(bf)
         cheb[r + 1, b] = following
         if r < DEG - 1:
@@ -314,42 +335,47 @@
         prepare(i, j)
     pack(0)
     pl.semaphore_wait(barrier, greeted)
+    send(0, x_sides)
     send(0, c_sides)
     send(0, z_sides)
-    send(0, x_sides)
-    for copy in fetches[3:]:
+    for copy in fetches[3:6]:
         copy.wait()
     factor = 2.0 / jnp.full((1, size), bound[0], f32)
-    for i, j in blocks:
-        tables(i, j)
     for r in range(DEG):
         if r == 0:
-            for k in range(tile_groups):
-                tile_copy(k).wait()
+            for k in range(GROUPS):
+                fetches[6 + k].wait()
+                some = [(i, j) for j in range(k * span, (k + 1) * span) for i in range(ex)]
+                for i, j in some:
+                    tables(i, j)
+                    weights(i, j)
+                for i, j in some:
+                    own_product(r, i, j)
+        else:
             for i, j in blocks:
-                weights(i, j)
-        for i, j in blocks:
-            own_product(r, i, j)
+                own_product(r, i, j)
         add_totals(r)
-        receive(r, x_sides)
+        if r == DEG - 1:
+            hear(r - 1)
+            tell(r)
+        receive_x(r)
         sent(r)
         unpack_x(r)
         for i, j in inner:
             advance(r, i, j)
-        receive(r, z_sides + c_sides)
+        receive_zc(r)
         if r > 0:
-            pl.semaphore_wait(know_sem.at[r - 1], len(JUMPS[r - 1]))
-        if r < len(JUMPS):
-            for dx in JUMPS[r]:
-                signal(know_sem.at[r], around(dx, 0))
+            hear(r if r == DEG - 1 else r - 1)
+        if r < DEG - 1:
+            tell(r)
         unpack_zc(r)
         for i, j in corners:
             advance(r, i, j)
         if r < DEG - 1:
             send(r + 1, c_sides)
-            send(r + 1, z_sides)
             pack(r + 1)
             send(r + 1, x_sides)
+            send(r + 1, z_sides)
 
     width = en_in.shape[2]
     if width > scales * chan:
@@ -373,7 +399,13 @@
             device_id_type=MESH,
         )
 
-    for py in range(ny):
+    for px in range(nx):
+
+        @pl.when(me != px * ny)
+        def _():
+            share(px, 0).start()
+
+    for py in range(1, ny):
 
         @pl.when(gy != py)
         def _():
@@ -402,7 +434,7 @@
     for s in range(scales):
         energy[s : s + 1, :] = total[:, s * chan : (s + 1) * chan]
     stores.append(pltpu.make_async_copy(energy, energy_out, sem.at[1]))
-    stores[-1].start()
+    stores[-1].start(priority=1)
     for store in stores:
         store.wait()
 
@@ -423,7 +455,7 @@
         bf, f32 = jnp.bfloat16, jnp.float32
         vmem = pl.BlockSpec(memory_space=pltpu.VMEM)
         hbm = pl.BlockSpec(memory_space=pltpu.HBM)
-        rows = [chan * (2 if r == 0 else 1) for r in range(DEG)]
+        rows = [chan + (8 if r == 0 else 0) for r in range(DEG)]
         made, shared = pl.pallas_call(
             functools.partial(kernel, nx, ny),
             out_shape=(
@@ -443,8 +475,8 @@
                 pltpu.SMEM((nb * slots,), f32),
                 pltpu.VMEM((ex, ey, slots, size, size), bf),
                 pltpu.VMEM((nb, 2 * size, size), bf),
-                [pltpu.VMEM((nb, 2 * chan, size), bf), pltpu.VMEM((nb, chan, size), bf)],
-                pltpu.VMEM((nb, 4 * chan, size), f32),
+                [pltpu.VMEM((nb, rows[k], size), bf) for k in range(2)],
+                pltpu.VMEM((nb, 2 * rows[0], size), f32),
                 pltpu.VMEM((nb, chan, size), f32),
                 pltpu.VMEM((DEG + 1, nb, chan, size), f32),
                 pltpu.VMEM((nb, 1, size), f32),
@@ -452,14 +484,12 @@
                 [pltpu.VMEM((ZERO + 1, rows[min(k, 1)], size), bf) for k in range(3)],
                 [pltpu.VMEM((2, quads, rows[r], size), bf) for r in range(DEG)],
                 [pltpu.VMEM((2, quads, rows[r], size), bf) for r in range(DEG)],
-                [pltpu.VMEM((2, ex, rows[r], size), bf) for r in range(DEG)],
-                [pltpu.VMEM((4, rows[r], size), bf) for r in range(DEG)],
-                pltpu.SemaphoreType.DMA((6,)),
-                pltpu.SemaphoreType.DMA((4,)),
-                pltpu.SemaphoreType.DMA((8,)),
-                pltpu.SemaphoreType.DMA((2, 8)),
+                [pltpu.VMEM((2 * ex + 4, rows[r], size), bf) for r in range(DEG)],
+                pltpu.SemaphoreType.DMA((3 + GROUPS,)),
+                pltpu.SemaphoreType.DMA((1,)),
+                pltpu.SemaphoreType.DMA((2, 2)),
                 pltpu.SemaphoreType.DMA((2,)),
-                pltpu.SemaphoreType.REGULAR((len(JUMPS),)),
+                pltpu.SemaphoreType.REGULAR((len(STEPS),)),
             ],
             compiler_params=pltpu.CompilerParams(
                 collective_id=0, has_side_effects=True, vmem_limit_bytes=VMEM_LIMIT

time: 32 us -> 31 us (0.969)
  Pallas kernels: 30.6 us -> 29.6 us
    pallas_call x1, Pallas kernels: 29.7 us -> 28.7 us  [shards(): pl.pallas_call(functools.partial(kernel, nx, ny), out_shape=(jax.ShapeDty...]
where the time goes in v3:
time: 31 us; the launch traced here: 30.9 us
  Pallas kernels  29.6 us (95%)
  between operations  1.29 us (4%)
    pallas_call x1, Pallas kernels, shards(): pl.pallas_call(functools.partial(kernel, nx, ny), out_shape=(jax.ShapeDty...  28.7 us
    pallas_call x1, Pallas kernels, shards(): pl.pallas_call(functools.partial(hand_out, n * nb * size), out_shape=(jax...  0.91 us

profile of v3, /device:TPU:1, one launch (start us, length us, event | category | flops | bytes accessed | tf_op | source)
XLA Modules:
  0.0 30.9 jit_solution(17749655553614816230)
XLA Ops:
  1.3 28.7 %shard_map.95 = (f32[6,2,8,16,128]{4,3,2,1,0:T(8,128)S(1)}, f32[128,1,128]{2,1,0:T(1,128)S(1)}) custom-call(f32[2,8,16,128]{3,2,1,0:T(8,128)} %sig_hbm.1, bf16[2,8,4,128,128]{4,3,2,1,0:T(8,128)(2,1)} %tiles_hbm.1, s32[2,4,8]{2,1,0:T(4,128)} %bitcast.2, s32[2,4,8]{2,1,0:T(4,128)} %bitcast.3, s32[2,8]{1,0:T(2,128)} %live_hbm.1, s32[2,8]{1,0:T(2,128)} %edge_hbm.1, ...), custom_call_target="tpu_custom_call" | custom-call | tf_op jit(solution)/shard_map/pallas_call | solution.py:459
  30.0 0.9 %shard_map.96 = (f32[6,2,8,16,128]{4,3,2,1,0:T(8,128)}, f32[6,16]{1,0:T(8,128)}) custom-call(f32[6,2,8,16,128]{4,3,2,1,0:T(8,128)S(1)} %get-tuple-element.4.made, f32[128,1,128]{2,1,0:T(1,128)S(1)} %get-tuple-element.5.shared), custom_call_target="tpu_custom_call" | custom-call | tf_op jit(solution)/shard_map/pallas_call | solution.py:506

commit v4 on v3

--- a/solution.py
+++ b/solution.py
@@ -12,6 +12,7 @@
 VMEM_LIMIT = 24 * 1024 * 1024
 MESH = pl.DeviceIdType.MESH
 NT = (((1,), (1,)), ((), ()))
+NN = (((1,), (0,)), ((), ()))
 SIDES = ((-1, 0), (1, 0), (0, -1), (0, 1), (-1, -1), (-1, 1), (1, -1), (1, 1))
 STEPS = (2, 4, 8, 16)
 GROUPS = 2
@@ -253,15 +254,18 @@
             index[b * slots + s] = jnp.where(jnp.logical_and(live, d != 4), at, ZERO)
             used[b * slots + s] = jnp.where(mine, 1.0, 0.0)
 
+    def turn(packed):
+        p = packed.astype(f32)
+        q = jnp.concatenate([p[:EDGE]] * groups, axis=0)
+        return jnp.concatenate([p.T.astype(bf), q.T.astype(bf)], axis=1)
+
     def weights(i, j):
         packed = None
         for s in range(slots):
-            tile = tiles[i, j, s]
-            term = (pltpu.roll(tile, s * EDGE, 1) if s else tile) * group[s]
-            packed = term if packed is None else packed + term
-        w_edge[flat(i, j), :size] = packed
-        for t in range(groups):
-            w_edge[flat(i, j), pl.ds(size + t * EDGE, EDGE)] = packed[:EDGE]
+            tile = tiles[i, j, s].astype(f32)
+            rolled = pltpu.roll(tile, s * EDGE, 1) if s else tile
+            packed = rolled if packed is None else jnp.where(lane >= s * EDGE, rolled, packed)
+        w_edge[flat(i, j)] = turn(packed)
 
     def own_product(r, i, j):
         b = flat(i, j)
@@ -290,8 +294,8 @@
         for s in range(slots):
             term = cells_of(r)[index[b * slots + s]] * group[s]
             picked = term if picked is None else picked + term
-        weight = w_edge[b] if r < DEG - 1 else w_edge[b, :size]
-        return lax.dot_general(picked, weight, NT, preferred_element_type=f32)
+        weight = w_edge[b] if r < DEG - 1 else w_edge[b, :, :size]
+        return lax.dot_general(picked, weight, NN, preferred_element_type=f32)
 
     def add_totals(k):
         for s in range(scales):
@@ -474,7 +478,7 @@
                 pltpu.SMEM((nb * slots,), jnp.int32),
                 pltpu.SMEM((nb * slots,), f32),
                 pltpu.VMEM((ex, ey, slots, size, size), bf),
-                pltpu.VMEM((nb, 2 * size, size), bf),
+                pltpu.VMEM((nb, size, 2 * size), bf),
                 [pltpu.VMEM((nb, rows[k], size), bf) for k in range(2)],
                 pltpu.VMEM((nb, 2 * rows[0], size), f32),
                 pltpu.VMEM((nb, chan, size), f32),

time: 31 us -> 30.8 us (level)
  no operation moved by 1% of the time
where the time goes in v4:
time: 30.8 us; the launch traced here: 30.7 us
  Pallas kernels  29.4 us (95%)
  between operations  1.29 us (4%)
    pallas_call x1, Pallas kernels, shards(): pl.pallas_call(functools.partial(kernel, nx, ny), out_shape=(jax.ShapeDty...  28.5 us
    pallas_call x1, Pallas kernels, shards(): pl.pallas_call(functools.partial(hand_out, n * nb * size), out_shape=(jax...  0.91 us

profile of v4, /device:TPU:1, one launch (start us, length us, event | category | flops | bytes accessed | tf_op | source)
XLA Modules:
  0.0 30.7 jit_solution(2792356059705151970)
XLA Ops:
  1.3 28.5 %shard_map.95 = (f32[6,2,8,16,128]{4,3,2,1,0:T(8,128)S(1)}, f32[128,1,128]{2,1,0:T(1,128)S(1)}) custom-call(f32[2,8,16,128]{3,2,1,0:T(8,128)} %sig_hbm.1, bf16[2,8,4,128,128]{4,3,2,1,0:T(8,128)(2,1)} %tiles_hbm.1, s32[2,4,8]{2,1,0:T(4,128)} %bitcast.2, s32[2,4,8]{2,1,0:T(4,128)} %bitcast.3, s32[2,8]{1,0:T(2,128)} %live_hbm.1, s32[2,8]{1,0:T(2,128)} %edge_hbm.1, ...), custom_call_target="tpu_custom_call" | custom-call | tf_op jit(solution)/shard_map/pallas_call | solution.py:463
  29.8 0.9 %shard_map.96 = (f32[6,2,8,16,128]{4,3,2,1,0:T(8,128)}, f32[6,16]{1,0:T(8,128)}) custom-call(f32[6,2,8,16,128]{4,3,2,1,0:T(8,128)S(1)} %get-tuple-element.4.made, f32[128,1,128]{2,1,0:T(1,128)S(1)} %get-tuple-element.5.shared), custom_call_target="tpu_custom_call" | custom-call | tf_op jit(solution)/shard_map/pallas_call | solution.py:510

commit v5 on v4

--- a/solution.py
+++ b/solution.py
@@ -67,15 +67,15 @@
     fetches = [
         pltpu.make_async_copy(src, dst, in_sem.at[k])
         for src, dst, k in (
-            (sig_hbm, sig, 0), (live_hbm, live_rows, 1), (edge_hbm, bound_rows, 1),
-            (tdir_hbm, tdir, 2), (tmask_hbm, tmask, 2), (coef_hbm, coef, 2),
+            (sig_hbm, sig, 0), (live_hbm, live_rows, 0), (edge_hbm, bound_rows, 0),
+            (tdir_hbm, tdir, 1), (tmask_hbm, tmask, 1), (coef_hbm, coef, 1),
         )
     ]
     span = ey // GROUPS
     for k in range(GROUPS):
         part = pl.ds(k * span, span)
         fetches.append(
-            pltpu.make_async_copy(tiles_hbm.at[:, part], tiles.at[:, part], in_sem.at[3 + k])
+            pltpu.make_async_copy(tiles_hbm.at[:, part], tiles.at[:, part], in_sem.at[1 + k])
         )
     def near(g, m, step=1):
         return (g >= step).astype(jnp.int32) + (g < m - step).astype(jnp.int32)
@@ -339,8 +339,8 @@
         prepare(i, j)
     pack(0)
     pl.semaphore_wait(barrier, greeted)
+    send(0, c_sides)
     send(0, x_sides)
-    send(0, c_sides)
     send(0, z_sides)
     for copy in fetches[3:6]:
         copy.wait()
@@ -397,8 +397,8 @@
         return pltpu.make_async_remote_copy(
             src_ref=en_in.at[me],
             dst_ref=en_in.at[me],
-            send_sem=en_sem.at[0],
-            recv_sem=en_sem.at[1],
+            send_sem=send_sem.at[0],
+            recv_sem=en_sem.at[0],
             device_id=(px, py),
             device_id_type=MESH,
         )
@@ -426,8 +426,8 @@
             totals[s, i, j] = totals[s, i, j] + c * cheb[DEG, flat(i, j)]
 
     rest = en_in.at[pl.ds(0, n - 1)]
-    pltpu.make_async_copy(rest, rest, en_sem.at[1]).wait()
     pltpu.make_async_copy(rest, rest, en_sem.at[0]).wait()
+    pltpu.make_async_copy(rest, rest, send_sem.at[0]).wait()
 
 
 def hand_out(count, made, shared, out_hbm, energy_out, energy, sem):
@@ -489,10 +489,10 @@
                 [pltpu.VMEM((2, quads, rows[r], size), bf) for r in range(DEG)],
                 [pltpu.VMEM((2, quads, rows[r], size), bf) for r in range(DEG)],
                 [pltpu.VMEM((2 * ex + 4, rows[r], size), bf) for r in range(DEG)],
-                pltpu.SemaphoreType.DMA((3 + GROUPS,)),
+                pltpu.SemaphoreType.DMA((1 + GROUPS,)),
                 pltpu.SemaphoreType.DMA((1,)),
                 pltpu.SemaphoreType.DMA((2, 2)),
-                pltpu.SemaphoreType.DMA((2,)),
+                pltpu.SemaphoreType.DMA((1,)),
                 pltpu.SemaphoreType.REGULAR((len(STEPS),)),
             ],
             compiler_params=pltpu.CompilerParams(

time: 30.8 us -> 30.7 us (level)
  no operation moved by 1% of the time
where the time goes in v5:
time: 30.7 us; the launch traced here: 30.6 us
  Pallas kernels  29.3 us (95%)
  between operations  1.29 us (4%)
    pallas_call x1, Pallas kernels, shards(): pl.pallas_call(functools.partial(kernel, nx, ny), out_shape=(jax.ShapeDty...  28.4 us
    pallas_call x1, Pallas kernels, shards(): pl.pallas_call(functools.partial(hand_out, n * nb * size), out_shape=(jax...  0.91 us

profile of v5, /device:TPU:1, one launch (start us, length us, event | category | flops | bytes accessed | tf_op | source)
XLA Modules:
  0.0 30.6 jit_solution(10176489351354009862)
XLA Ops:
  1.3 28.4 %shard_map.95 = (f32[6,2,8,16,128]{4,3,2,1,0:T(8,128)S(1)}, f32[128,1,128]{2,1,0:T(1,128)S(1)}) custom-call(f32[2,8,16,128]{3,2,1,0:T(8,128)} %sig_hbm.1, bf16[2,8,4,128,128]{4,3,2,1,0:T(8,128)(2,1)} %tiles_hbm.1, s32[2,4,8]{2,1,0:T(4,128)} %bitcast.2, s32[2,4,8]{2,1,0:T(4,128)} %bitcast.3, s32[2,8]{1,0:T(2,128)} %live_hbm.1, s32[2,8]{1,0:T(2,128)} %edge_hbm.1, ...), custom_call_target="tpu_custom_call" | custom-call | tf_op jit(solution)/shard_map/pallas_call | solution.py:463
  29.7 0.9 %shard_map.96 = (f32[6,2,8,16,128]{4,3,2,1,0:T(8,128)}, f32[6,16]{1,0:T(8,128)}) custom-call(f32[6,2,8,16,128]{4,3,2,1,0:T(8,128)S(1)} %get-tuple-element.4.made, f32[128,1,128]{2,1,0:T(1,128)S(1)} %get-tuple-element.5.shared), custom_call_target="tpu_custom_call" | custom-call | tf_op jit(solution)/shard_map/pallas_call | solution.py:510

commit v6 on v5

--- a/solution.py
+++ b/solution.py
@@ -91,8 +91,7 @@
         pl.semaphore_wait(know_sem.at[k], near(gx, nx, STEPS[k]))
 
     greeted = (1 + near(gx, nx)) * (1 + near(gy, ny)) - 1
-    for copy in fetches[:3]:
-        copy.start()
+    fetches[0].start()
     barrier = pltpu.get_barrier_semaphore()
     for dx, dy in SIDES:
 
@@ -100,7 +99,7 @@
         def _():
             signal(barrier, (gx + dx, gy + dy))
 
-    for copy in fetches[3:]:
+    for copy in fetches[1:]:
         copy.start()
     for k, (dx, dy) in enumerate(SIDES):
 
@@ -359,7 +358,7 @@
             for i, j in blocks:
                 own_product(r, i, j)
         add_totals(r)
-        if r == DEG - 1:
+        if r == DEG - 2:
             hear(r - 1)
             tell(r)
         receive_x(r)
@@ -369,9 +368,9 @@
             advance(r, i, j)
         receive_zc(r)
         if r > 0:
-            hear(r if r == DEG - 1 else r - 1)
+            hear(r - 1 if r == 1 else r)
         if r < DEG - 1:
-            tell(r)
+            tell(r + 1 if r == DEG - 2 else r)
         unpack_zc(r)
         for i, j in corners:
             advance(r, i, j)

time: 30.7 us -> 30.7 us (level)
  no operation moved by 1% of the time
where the time goes in v6:
time: 30.7 us; the launch traced here: 30.6 us
  Pallas kernels  29.3 us (95%)
  between operations  1.29 us (4%)
    pallas_call x1, Pallas kernels, shards(): pl.pallas_call(functools.partial(kernel, nx, ny), out_shape=(jax.ShapeDty...  28.4 us
    pallas_call x1, Pallas kernels, shards(): pl.pallas_call(functools.partial(hand_out, n * nb * size), out_shape=(jax...  0.91 us

profile of v6, /device:TPU:1, one launch (start us, length us, event | category | flops | bytes accessed | tf_op | source)
XLA Modules:
  0.0 30.6 jit_solution(6157720738710258592)
XLA Ops:
  1.3 28.4 %shard_map.95 = (f32[6,2,8,16,128]{4,3,2,1,0:T(8,128)S(1)}, f32[128,1,128]{2,1,0:T(1,128)S(1)}) custom-call(f32[2,8,16,128]{3,2,1,0:T(8,128)} %sig_hbm.1, bf16[2,8,4,128,128]{4,3,2,1,0:T(8,128)(2,1)} %tiles_hbm.1, s32[2,4,8]{2,1,0:T(4,128)} %bitcast.2, s32[2,4,8]{2,1,0:T(4,128)} %bitcast.3, s32[2,8]{1,0:T(2,128)} %live_hbm.1, s32[2,8]{1,0:T(2,128)} %edge_hbm.1, ...), custom_call_target="tpu_custom_call" | custom-call | tf_op jit(solution)/shard_map/pallas_call | solution.py:462
  29.7 0.9 %shard_map.96 = (f32[6,2,8,16,128]{4,3,2,1,0:T(8,128)}, f32[6,16]{1,0:T(8,128)}) custom-call(f32[6,2,8,16,128]{4,3,2,1,0:T(8,128)S(1)} %get-tuple-element.4.made, f32[128,1,128]{2,1,0:T(1,128)S(1)} %get-tuple-element.5.shared), custom_call_target="tpu_custom_call" | custom-call | tf_op jit(solution)/shard_map/pallas_call | solution.py:509
